TPU v7x, 256 devices: a whole 4x4x8 slice. The times are simulated.
256 devices in a mesh: dp: 8 (over x, z_lo), owner: 32 (over y, z_hi, core).
Axes of the slice: x: 4, y: 4, z: 8 (z_hi: 4, z_lo: 2; z = z_hi * 2 + z_lo), core: 2. Of those that a mesh axis runs over, the one named last changes fastest.
Arguments:
- partial_grads: bfloat16 [8, 48, 1024, 1024], P('dp', None, 'owner'), may hold values from -2.09375 to 2.09375
- owner_map: int32 [48], replicated, may hold values from 0 to 31, as said below
- left_stats: float32 [32, 3, 1024, 1024], P('owner', None, 'dp'), may hold values from -1.8 to 1.8
- right_stats: float32 [32, 3, 1024, 1024], P('owner', None, 'dp'), may hold values from -1.8 to 1.8
- left_roots: bfloat16 [32, 3, 1024, 1024], P('owner', None, 'dp'), as said below
- right_roots: bfloat16 [32, 3, 1024, 1024], P('owner', None, 'dp'), as said below
Outputs:
- direction: bfloat16 [48, 1024, 1024], P(None, ('dp', 'owner'))
- new_left_stats: float32 [32, 3, 1024, 1024], P('owner', None, 'dp')
- new_right_stats: float32 [32, 3, 1024, 1024], P('owner', None, 'dp')
Inputs may be any that keep to these rules, and one draw needn't show every extreme that they name: `owner_map`: no owner index holds more than 3 blocks, and some owner holds exactly 3. `left_roots`: each block is dense and not symmetric; its diagonal entries are of order one and its off-diagonal entries are small. `right_roots`: each block is dense and not symmetric; its diagonal entries are of order one and its off-diagonal entries are small.
All inputs are finite; a program needn't handle non-finite values.
Results may differ from a plain program's by a relative error of at most 0.017.
Values may be sent and summed in bfloat16 or wider, within the bound.
A program may use at most 128 MiB of HBM per device.

v0:
```python
import jax
import jax.numpy as jnp
from jax import lax
from jax.sharding import Mesh
from jax.sharding import PartitionSpec as P

D_MODEL = 2560
D_IN = 10576
D_INNER = 5120
TILE = 1024
OWNER = ("owner_0", "owner_1", "owner_2")
DP = ("dp_0", "dp_1")
DP_OWNER = ("dp_0", "dp_1", "owner_0", "owner_1", "owner_2")


stat_decay = 0.999


def cut_along(array, dim, count):
    before, after = (array.shape[:dim], array.shape[dim + 1 :])
    return jnp.moveaxis(array.reshape(*before, count, -1, *after), dim, 0)


def summed_on_arrival(array, axis, dim):
    parts = cut_along(array, dim, lax.axis_size(axis))
    arrived = lax.all_to_all(parts, axis, split_axis=0, concat_axis=0, tiled=True)
    return arrived.astype(jnp.float32).sum(axis=0)


def gather_axes(array, axes, dim):
    if not axes:
        return array
    nearer = lax.all_gather(array, axes[-1], axis=dim, tiled=True)
    return gather_axes(nearer, axes[:-1], dim)


def laid_out(parts, dim):
    parts = jnp.moveaxis(parts, 0, dim)
    lengths = parts.shape
    return parts.reshape(*lengths[:dim], lengths[dim] * lengths[dim + 1], *lengths[dim + 2 :])


def moved_by_axis(parts, axes, turns):
    lengths = [lax.axis_size(a) for a in axes]
    parts = parts.reshape(*lengths, *parts.shape[1:])
    for k in turns:
        parts = lax.all_to_all(parts, axes[k], split_axis=k, concat_axis=k, tiled=True)
    return parts.reshape(-1, *parts.shape[len(axes) :])


def core_and_chips(array, groups, turns, split_dim, concat_dim):
    count = lax.axis_size(groups[0]) * lax.axis_size(groups[1])
    parts = cut_along(array, split_dim, count)
    return laid_out(moved_by_axis(parts, groups, turns), concat_dim)


def extents(count):
    index = jnp.arange(count, dtype=jnp.int32)
    in_cols = -(-D_IN // TILE)
    out_cols = -(-D_MODEL // TILE)
    in_count = -(-D_MODEL // TILE) * in_cols
    is_in = index < in_count
    other = jnp.maximum(index - in_count, 0)
    rows = jnp.where(
        is_in,
        jnp.minimum(TILE, D_MODEL - index // in_cols * TILE),
        jnp.minimum(TILE, D_INNER - other // out_cols * TILE),
    )
    cols = jnp.where(
        is_in,
        jnp.minimum(TILE, D_IN - index % in_cols * TILE),
        jnp.minimum(TILE, D_MODEL - other % out_cols * TILE),
    )
    return (rows, cols)


def body(partial_grads, owner_map, left_stats, right_stats, left_roots, right_roots):
    owners = lax.axis_size(OWNER)
    owner_here = lax.axis_index(OWNER)
    dp_here = lax.axis_index(DP)
    tiles = owner_map.shape[0]
    slots = left_stats.shape[1]
    lanes = left_stats.shape[2]
    tile = left_stats.shape[3]
    piece = partial_grads.shape[2]
    rows, cols = extents(tiles)
    line = jnp.arange(tile, dtype=jnp.int32)
    piece_rows = owner_here * piece + jnp.arange(piece, dtype=jnp.int32)
    source_mask = (piece_rows[None, :, None] < rows[:, None, None]) & (
        line[None, None, :] < cols[:, None, None]
    )
    local = jnp.where(source_mask, partial_grads[0], jnp.zeros((), jnp.bfloat16))
    ids = jnp.arange(tiles, dtype=jnp.int32)
    same = (owner_map[:, None] == owner_map[None, :]) & (ids[None, :] < ids[:, None])
    slot = jnp.sum(same.astype(jnp.int32), axis=1)
    picks = (slot[None, None, :] == jnp.arange(slots, dtype=jnp.int32)[:, None, None]) & (
        owner_map[None, None, :] == jnp.arange(owners, dtype=jnp.int32)[None, :, None]
    )
    tile_of = jnp.sum(jnp.where(picks, ids[None, None, :], 0), axis=2)
    filled = jnp.any(picks, axis=2)
    shares = summed_on_arrival(local.astype(jnp.float32).astype(jnp.bfloat16), DP, 1).astype(
        jnp.bfloat16
    )
    taken = jnp.take(shares, tile_of.reshape(-1), axis=0)
    taken = taken.reshape((slots, owners) + shares.shape[1:])
    arrived = lax.all_to_all(
        jnp.where(filled[:, :, None, None], taken, jnp.zeros((), shares.dtype)),
        OWNER,
        split_axis=1,
        concat_axis=1,
        tiled=True,
    )
    grads = gather_axes(arrived, DP, 2).reshape(slots, tile, tile)
    grad_rows = lax.dynamic_slice_in_dim(grads, dp_here * lanes, lanes, 1)
    grad_cols = lax.dynamic_slice_in_dim(grads, dp_here * lanes, lanes, 2)
    left_gram = jnp.einsum("srk,stk->srt", grad_rows, grads, preferred_element_type=jnp.float32)
    right_gram = jnp.einsum("skc,skt->sct", grad_cols, grads, preferred_element_type=jnp.float32)
    new_left = stat_decay * left_stats[0] + (1.0 - stat_decay) * left_gram
    new_right = stat_decay * right_stats[0] + (1.0 - stat_decay) * right_gram
    left_part = jnp.einsum(
        "srk,skc->src", left_roots[0], grads, preferred_element_type=jnp.float32
    ).astype(jnp.bfloat16)
    product = jnp.einsum(
        "srk,skc->src",
        left_part,
        gather_axes(right_roots[0], DP, 1),
        preferred_element_type=jnp.float32,
    )
    tile_here = lax.dynamic_index_in_dim(tile_of, owner_here, 1, keepdims=False)
    rows_here = jnp.take(rows, tile_here)
    cols_here = jnp.take(cols, tile_here)
    block_rows = dp_here * lanes + jnp.arange(lanes, dtype=jnp.int32)
    out_mask = (block_rows[None, :, None] < rows_here[:, None, None]) & (
        line[None, None, :] < cols_here[:, None, None]
    )
    result = jnp.where(out_mask, product, jnp.float32(0.0)).astype(jnp.bfloat16)
    sub_rows = lanes // owners
    returned = core_and_chips(
        result.reshape(slots, owners, sub_rows, tile),
        (("owner_0", "owner_1"), "owner_2"),
        (1, 0),
        1,
        1,
    )
    flat = returned.reshape(slots * owners, sub_rows, tile)
    direction = jnp.take(flat, slot * owners + owner_map, axis=0)
    return (direction, new_left[None], new_right[None])


def solution(mesh):
    torus = Mesh(
        mesh.devices.reshape(4, 2, 4, 4, 2), ("dp_0", "dp_1", "owner_0", "owner_1", "owner_2")
    )
    in_specs = (
        P(DP, None, OWNER, None),
        P(),
        P(OWNER, None, DP, None),
        P(OWNER, None, DP, None),
        P(OWNER, None, DP, None),
        P(OWNER, None, DP, None),
    )
    out_specs = (P(None, DP_OWNER, None), P(OWNER, None, DP, None), P(OWNER, None, DP, None))
    return jax.shard_map(body, mesh=torus, in_specs=in_specs, out_specs=out_specs, check_vma=False)
```

profile of v0, /device:TPU:1, one launch (start us, length us, event | category | flops | bytes accessed | tf_op | source)
XLA Modules:
  0.0 344.5 jit_solution(3709839346918346826)
XLA Ops:
  7.2 0.0 copy-start
  7.2 0.1 iota_compare_fusion
  7.3 3.7 %copy.46 = bf16[1,48,32,1024]{3,1,2,0:T(8,128)(2,1)S(1)} copy(bf16[1,48,32,1024]{3,2,1,0:T(8,128)(2,1)} %param.8) | data formatting | bytes 6291456 | tf_op args[0]
  11.0 0.1 broadcast_compare_fusion
  11.1 1.1 fusion.2
  12.2 4.1 %copy.47 = bf16[8,48,4,1024]{3,2,1,0:T(4,128)(2,1)} copy(bf16[8,48,4,1024]{3,1,2,0:T(8,128)(2,1)S(1)} %fusion.2) | data formatting | bytes 6291456 | tf_op jit(solution)/shard_map/transpose | solution.py:21
  16.3 0.0 copy-start.2
  16.3 6.3 %all-to-all-start = ((bf16[8,48,4,1024]{3,2,1,0:T(4,128)(2,1)}), bf16[8,48,4,1024]{3,2,1,0:T(4,128)(2,1)}, u32[]{:S(2)}, u32[]{:S(2)}) async-start(bf16[8,48,4,1024]{3,2,1,0:T(4,128)(2,1)} %copy.47), calls=%async_computation | async-start | bytes 6291456 | tf_op jit(solution)/shard_map/all_to_all | solution.py:26
  22.7 0.0 all-gather.11.cloned.1.call-start
  22.7 0.7 all-gather.11.cloned.1.call-update
  23.4 0.0 all-gather.7.cloned.1.call-start
  23.4 0.0 copy-done.2
  23.4 0.2 convert_reduce_fusion
  23.7 0.2 fusion.12
  23.8 0.1 reshape.289
  23.9 0.2 and_reduce_fusion
  24.1 49.4 %all-to-all-done = bf16[8,48,4,1024]{3,2,1,0:T(4,128)(2,1)} async-done(((bf16[8,48,4,1024]{3,2,1,0:T(4,128)(2,1)}), bf16[8,48,4,1024]{3,2,1,0:T(4,128)(2,1)}, u32[]{:S(2)}, u32[]{:S(2)}) %all-to-all-start) | async-done | bytes 3145760 | tf_op jit(solution)/shard_map/all_to_all | solution.py:26
  73.5 3.4 reduce_sum.32
  76.9 1.2 gather_fusion
  78.1 0.2 copy.48
  78.4 0.2 select_select_fusion
  78.6 0.6 copy.49
  79.2 37.8 %all_to_all.20 = bf16[3,32,4,1024]{3,2,0,1:T(4,128)(2,1)S(1)} all-to-all(bf16[3,32,4,1024]{3,2,0,1:T(4,128)(2,1)S(1)} %copy.49), channel_id=1, replica_groups=mesh['dp_0'=4,'dp_1'=2,'owner_0'=4,'owner_1'=4,'owner_2'=2] {'owner_0','..., dimensions={1} | all-to-all | bytes 1572864 | tf_op jit(solution)/shard_map/all_to_all | solution.py:106
  117.0 1.1 copy.50
  118.1 0.0 all-gather.7.cloned.1.call-update
  118.1 0.0 all-gather.13.cloned.1.call-start
  118.2 0.0 all-gather.11.cloned.1.call-done
  118.2 0.7 all-gather.13.cloned.1.call-update
  118.9 0.2 all-gather.9.cloned.1.call-start
  119.1 26.8 %all-gather.7.cloned.1.call-done = bf16[3,32,8,1024]{3,1,0,2:T(8,128)(2,1)} async-done(((bf16[3,32,4,1024]{3,1,0,2:T(8,128)(2,1)}), bf16[3,32,8,1024]{3,1,0,2:T(8,128)(2,1)}) %all-gather.7.cloned.1.call-update) | async-done | bytes 1572880 | tf_op jit(solution)/shard_map/all_gather | solution.py:33
  145.9 3.4 copy.51
  149.3 0.0 all-gather.9.cloned.1.call-update
  149.3 0.2 dynamic-slice_reduce_fusion
  149.5 0.6 gather_fusion.3
  150.1 0.6 gather_fusion.2
  150.8 0.1 broadcast_compare_fusion.1
  150.9 0.1 iota_compare_fusion.2
  150.9 65.3 %all-gather.13.cloned.1.call-done = bf16[1,3,1024,1024]{3,2,1,0:T(8,128)(2,1)} async-done(((bf16[1,3,256,1024]{3,2,1,0:T(8,128)(2,1)}), bf16[1,3,1024,1024]{3,2,1,0:T(8,128)(2,1)}) %all-gather.13.cloned.1.call-update) | async-done | bytes 6291472 | tf_op jit(solution)/shard_map/all_gather | solution.py:33
  216.3 71.1 %all-gather.9.cloned.1.call-done = bf16[3,32,32,1024]{3,2,1,0:T(8,128)(2,1)} async-done(((bf16[3,32,8,1024]{3,2,1,0:T(8,128)(2,1)}), bf16[3,32,32,1024]{3,2,1,0:T(8,128)(2,1)}) %all-gather.9.cloned.1.call-update) | async-done | bytes 6291472 | tf_op jit(solution)/shard_map/all_gather | solution.py:33
  287.4 0.0 copy-done
  287.4 7.8 %select_convert_fusion = bf16[3,128,1024]{2,1,0:T(8,128)(2,1)S(1)} fusion(bf16[1,3,1024,1024]{3,2,1,0:T(8,128)(2,1)} %all-gather.13.cloned.1.call-done, pred[3,1024]{1,0:T(4,128)(4,1)S(1)} %iota_compare_fusion.2, pred[3,128]{1,0:T(4,128)(4,1)S(1)} %broadcast_compare_fusion.1, bf16[3,1024,1024]{2,1,0:T(8,128)(2,1)} %bitcast.39, ...), kind=kOutput, calls=%fused_computation.12 | convolution fusion | flops 1612185600 | bytes 14159232 | tf_op jit(solution)/shard_map/srk,skc->src/dot_general | solution.py:123
  295.2 0.3 reshape_reshape.6
  295.5 0.3 copy.54
  295.8 0.3 copy.55
  296.1 4.8 %all_to_all.21 = bf16[16,2,3,1,4,1024]{5,4,0,2,3,1:T(4,128)(2,1)S(1)} all-to-all(bf16[16,2,3,1,4,1024]{5,4,0,2,3,1:T(4,128)(2,1)S(1)} %copy.55), channel_id=1, replica_groups=mesh['dp_0'=4,'dp_1'=2,'owner_0'=4,'owner_1'=4,'owner_2'=2] {'owner_2'}, dimensions={1} | all-to-all | bytes 1572864 | tf_op jit(solution)/shard_map/all_to_all | solution.py:47
  300.9 0.0 slice-start
  300.9 1.3 copy.56
  302.3 9.3 %all-to-all-start.3 = ((bf16[16,2,3,1,4,1024]{5,4,1,2,3,0:T(4,128)(2,1)}), bf16[16,2,3,1,4,1024]{5,4,1,2,3,0:T(4,128)(2,1)}, u32[]{:S(2)}, u32[]{:S(2)}) async-start(bf16[16,2,3,1,4,1024]{5,4,1,2,3,0:T(4,128)(2,1)} %copy.56), calls=%async_computation.3 | async-start | bytes 1572864 | tf_op jit(solution)/shard_map/all_to_all | solution.py:47
  311.6 0.0 slice-start.1
  311.6 0.0 copy-start.1
  311.6 6.0 %fusion.3 = f32[1,3,128,1024]{3,2,1,0:T(8,128)} fusion(f32[1,3,128,1024]{3,2,1,0:T(8,128)} %param.11, bf16[3,1024,1024]{2,1,0:T(8,128)(2,1)} %bitcast.40, s32[]{:T(128)S(6)} %select_n.139), kind=kOutput, calls=%fused_computation.9 | convolution fusion | flops 806486016 | bytes 10223620 | tf_op jit(solution)/shard_map/skc,skt->sct/dot_general | solution.py:117
  317.7 0.0 slice-done
  317.7 0.0 slice-done.1
  317.7 0.0 copy-done.1
  317.7 3.4 fusion.4
  321.1 13.2 %all-to-all-done.3 = bf16[16,2,3,1,4,1024]{5,4,1,2,3,0:T(4,128)(2,1)} async-done(((bf16[16,2,3,1,4,1024]{5,4,1,2,3,0:T(4,128)(2,1)}), bf16[16,2,3,1,4,1024]{5,4,1,2,3,0:T(4,128)(2,1)}, u32[]{:S(2)}, u32[]{:S(2)}) %all-to-all-start.3) | async-done | bytes 786464 | tf_op jit(solution)/shard_map/all_to_all | solution.py:47
  334.3 1.5 copy.57
  335.8 0.3 copy.58
  336.1 0.9 gather_fusion.1
  337.0 1.0 broadcast_select_fusion
  (14 shorter events, 0.1 us)
Async XLA Ops:
  7.2 280.2 %copy-start = (bf16[1,3,128,1024]{3,2,1,0:T(8,128)(2,1)S(1)}, bf16[1,3,128,1024]{3,2,1,0:T(8,128)(2,1)}, u32[]{:S(2)}) copy-start(bf16[1,3,128,1024]{3,2,1,0:T(8,128)(2,1)} %param.12) | copy-start | bytes 2359300
  16.3 7.1 %copy-start.2 = (s32[48]{0:T(128)S(1)}, s32[48]{0:T(128)}, u32[]{:S(2)}) copy-start(s32[48]{0:T(128)} %param.9) | copy-start | bytes 580
  16.3 57.1 %all-to-all-start = ((bf16[8,48,4,1024]{3,2,1,0:T(4,128)(2,1)}), bf16[8,48,4,1024]{3,2,1,0:T(4,128)(2,1)}, u32[]{:S(2)}, u32[]{:S(2)}) async-start(bf16[8,48,4,1024]{3,2,1,0:T(4,128)(2,1)} %copy.47), calls=%async_computation | async-start | bytes 6291456 | tf_op jit(solution)/shard_map/all_to_all | solution.py:26
  22.7 95.5 %all-gather.11.cloned.1.call-start = ((), (), s32[]{:S(2)}) async-start(), calls=%async_computation.6 | async-start | bytes 2359296 | tf_op jit(solution)/shard_map/all_gather | solution.py:33
  23.4 122.5 %all-gather.7.cloned.1.call-start = ((), (), s32[]{:S(2)}) async-start(), calls=%async_computation.4 | async-start | bytes 2359296 | tf_op jit(solution)/shard_map/all_gather | solution.py:33
  118.1 98.1 %all-gather.13.cloned.1.call-start = ((), (), s32[]{:S(2)}) async-start(), calls=%async_computation.7 | async-start | bytes 7864320 | tf_op jit(solution)/shard_map/all_gather | solution.py:33
  118.9 168.5 %all-gather.9.cloned.1.call-start = ((), (), s32[]{:S(2)}) async-start(), calls=%async_computation.5 | async-start | bytes 7864320 | tf_op jit(solution)/shard_map/all_gather | solution.py:33
  300.9 16.7 %slice-start = ((s8[6291456]{0:T(1024)(128)(4,1)}), s8[2097152]{0:T(1024)(128)(4,1)S(1)}, s32[]{:S(2)}) async-start(s8[6291456]{0:T(1024)(128)(4,1)} %bitcast.41), calls=%async_computation.8 | async-start | bytes 4194304
  302.3 32.1 %all-to-all-start.3 = ((bf16[16,2,3,1,4,1024]{5,4,1,2,3,0:T(4,128)(2,1)}), bf16[16,2,3,1,4,1024]{5,4,1,2,3,0:T(4,128)(2,1)}, u32[]{:S(2)}, u32[]{:S(2)}) async-start(bf16[16,2,3,1,4,1024]{5,4,1,2,3,0:T(4,128)(2,1)} %copy.56), calls=%async_computation.3 | async-start | bytes 1572864 | tf_op jit(solution)/shard_map/all_to_all | solution.py:47
  311.6 6.1 %slice-start.1 = ((s8[6291456]{0:T(1024)(128)(4,1)}), s8[4194304]{0:T(1024)(128)(4,1)S(1)}, s32[]{:S(2)}) async-start(s8[6291456]{0:T(1024)(128)(4,1)} %bitcast.41), calls=%async_computation.9 | async-start | bytes 8388608
  311.6 6.1 %copy-start.1 = (f32[1,3,128,1024]{3,2,1,0:T(8,128)S(1)}, f32[1,3,128,1024]{3,2,1,0:T(8,128)}, u32[]{:S(2)}) copy-start(f32[1,3,128,1024]{3,2,1,0:T(8,128)} %param.10) | copy-start | bytes 4718596
Sparse Core Ops, SparseCore 0:
  25.3 50.6 all-gather.10
  118.2 27.5 all-gather.6
  147.7 68.5 all-gather.12
  218.5 68.8 all-gather.8
where the time goes:
time: 346 us; the launch traced here: 345 us
  waiting for transfers between devices  227 us (66%)
  blocking collectives  42.6 us (12%)
  local copies, waits for them, and re-layouts  20.8 us (6%)
  matrix products  17.3 us (5%)
  starting transfers between devices  16 us (5%)
  between operations  14 us (4%)
  other arithmetic  6.64 us (2%)
    all_gather x4, waiting for transfers between devices, gather_axes(): nearer = lax.all_gather(array, axes[-1], axis=dim, tiled=True)  163 us
    all_to_all x1, waiting for transfers between devices, summed_on_arrival(): lax.all_to_all(parts, axis, split_axis=0, concat_axis=0, tiled=True)  49.4 us
    all_to_all x1, blocking collectives, body(): lax.all_to_all(jnp.where(filled[:, :, None, None], taken, jnp.zeros((), s...  37.8 us
    all_to_all x1, waiting for transfers between devices, moved_by_axis(): lax.all_to_all(parts, axes[k], split_axis=k, concat_axis=k, tiled=True)  13.2 us
    all_to_all x1, starting transfers between devices, moved_by_axis(): lax.all_to_all(parts, axes[k], split_axis=k, concat_axis=k, tiled=True)  9.33 us
    dot_general x1, matrix products, body(): jnp.einsum('srk,skc->src', left_part, gather_axes(right_roots[0], DP, 1),...  7.82 us
  transfers between devices with their start and end apart: 6, of which 5 were waited for; matrix products, arithmetic and copies ran while one was open for 6% of the time, Pallas kernels for 0%

commit v1 on v0

v1 whole, which is shorter than its diff:
```python
import jax
import jax.numpy as jnp
from jax import lax
from jax.experimental import pallas as pl
from jax.experimental.pallas import tpu as pltpu
from jax.sharding import Mesh
from jax.sharding import PartitionSpec as P

D_MODEL = 2560
D_IN = 10576
D_INNER = 5120
TILE = 1024
TILES = 48
OWNERS = 32
SLOTS = 3
PIECE = 32
LANES = 128
COLS = 128
HALF = 512
CHUNKS = 4
PER = TILES // CHUNKS
OWNER = ("owner_0", "owner_1", "owner_2")
DP = ("dp_0", "dp_1")
DP_OWNER = ("dp_0", "dp_1", "owner_0", "owner_1", "owner_2")
MESH = pl.DeviceIdType.MESH
F32 = jnp.float32
BF16 = jnp.bfloat16

stat_decay = 0.999


def extent(t):
    in_cols = -(-D_IN // TILE)
    out_cols = -(-D_MODEL // TILE)
    in_count = -(-D_MODEL // TILE) * in_cols
    other = jnp.maximum(t - in_count, 0)
    is_in = t < in_count
    rows = jnp.where(
        is_in,
        jnp.minimum(TILE, D_MODEL - t // in_cols * TILE),
        jnp.minimum(TILE, D_INNER - other // out_cols * TILE),
    )
    cols = jnp.where(
        is_in,
        jnp.minimum(TILE, D_IN - t % in_cols * TILE),
        jnp.minimum(TILE, D_MODEL - other % out_cols * TILE),
    )
    return rows, cols


class Ids:
    def __init__(self):
        self.n = 0

    def __call__(self, *shape):
        size = 1
        for s in shape:
            size *= s
        base = self.n
        self.n += size

        def at(*index):
            flat = 0
            for i, s in zip(index, shape):
                flat = flat * s + i
            return base + flat

        return at


IDS = Ids()
FAR = IDS(CHUNKS, 2)
NEAR = IDS(CHUNKS, 2)
CHAIN = IDS(CHUNKS, 2)
ZZ = IDS(CHUNKS)
RZ = IDS(SLOTS)
RN = IDS(SLOTS, 2)
RF = IDS(SLOTS, 2)
LZ = IDS(SLOTS)
A2A = IDS(SLOTS)
GZ = IDS(SLOTS)
GN = IDS(SLOTS, 2, 2)
GF = IDS(SLOTS, 2)
RET = IDS(SLOTS)
N_SEMS = IDS.n
LOC = Ids()
L_PG = LOC(CHUNKS)
L_R = LOC(SLOTS)
L_L = LOC(SLOTS)
L_LS = LOC(1)
L_RS = LOC(1)
L_NL = LOC(SLOTS)
L_NR = LOC(SLOTS)
N_LOC = LOC.n


def kernel(
    tile_s,
    place_s,
    pg_h,
    l_h,
    r_h,
    ls_h,
    rs_h,
    dir_o,
    nl_h,
    nr_h,
    pg,
    far,
    chs,
    near,
    ch,
    hs,
    zrecv,
    shares,
    staged,
    gf,
    rf,
    lp,
    ls,
    rs,
    nl,
    nr,
    gt,
    tp,
    obuf,
    ostage,
    ret,
    send,
    recv,
    local,
):
    x = lax.axis_index("dp_0")
    zl = lax.axis_index("dp_1")
    y = lax.axis_index("owner_0")
    zh = lax.axis_index("owner_1")
    co = lax.axis_index("owner_2")
    me = (y * 4 + zh) * 2 + co
    d = x * 2 + zl
    xp = (x + 1) % 4
    xm = (x + 3) % 4
    x2 = (x + 2) % 4
    zo = 1 - zl
    here = zl * 32 + me
    to_xp = {"dp_0": xp}
    to_xm = {"dp_0": xm}
    to_z = {"dp_1": zo}

    def owner_device(i):
        return {"owner_0": i // 8, "owner_1": (i // 2) % 4, "owner_2": i % 2}

    def any_device(i):
        return {
            "dp_1": i // 32,
            "owner_0": (i // 8) % 4,
            "owner_1": (i // 2) % 4,
            "owner_2": i % 2,
        }

    sent = []

    def start(src, dst, sem, device):
        copy = pltpu.make_async_remote_copy(
            src_ref=src,
            dst_ref=dst,
            send_sem=send.at[sem],
            recv_sem=recv.at[sem],
            device_id=device,
            device_id_type=MESH,
        )
        copy.start()
        sent.append(copy)

    def arrived(dst, sem):
        pltpu.make_async_remote_copy(
            src_ref=dst,
            dst_ref=dst,
            send_sem=send.at[sem],
            recv_sem=recv.at[sem],
            device_id=to_xp,
            device_id_type=MESH,
        ).wait_recv()

    def lanes(block, width=COLS):
        return pl.ds(pl.multiple_of(block * width, width), width)

    def chunk(k):
        return pl.ds(k * PER, PER)

    pg_in = [
        pltpu.make_async_copy(pg_h.at[chunk(k)], pg.at[chunk(k)], local.at[L_PG(k)])
        for k in range(CHUNKS)
    ]
    for copy in pg_in:
        copy.start()
    own_rows = pl.ds(pl.multiple_of(d * LANES, LANES), LANES)
    pair_rows = pl.ds(pl.multiple_of(zl * LANES, LANES), LANES)
    r_in = [
        pltpu.make_async_copy(
            r_h.at[s, :, lanes(zl, HALF)], rf.at[s, own_rows, :], local.at[L_R(s)]
        )
        for s in range(SLOTS)
    ]
    l_in = [
        pltpu.make_async_copy(l_h.at[s], lp.at[s, pair_rows, :], local.at[L_L(s)])
        for s in range(SLOTS)
    ]
    ls_in = pltpu.make_async_copy(ls_h, ls, local.at[L_LS(0)])
    rs_in = pltpu.make_async_copy(rs_h, rs, local.at[L_RS(0)])
    for copy in (*r_in, *l_in, ls_in, rs_in):
        copy.start()

    barrier = pltpu.get_barrier_semaphore()
    pl.semaphore_signal(barrier, inc=1, device_id=to_xp, device_id_type=MESH)
    pl.semaphore_signal(barrier, inc=1, device_id=to_xm, device_id_type=MESH)

    def greet(k, carry):
        pl.semaphore_signal(
            barrier, inc=1, device_id=any_device((here + k) % 64), device_id_type=MESH
        )
        return carry

    lax.fori_loop(1, 64, greet, 0)
    pl.semaphore_wait(barrier, 65)

    def send_near(k):
        start(pg.at[chunk(k), :, lanes(xp)], near.at[0, chunk(k)], NEAR(k, 0), to_xp)
        start(pg.at[chunk(k), :, lanes(4 + xm)], near.at[1, chunk(k)], NEAR(k, 1), to_xm)

    for k in range(CHUNKS):
        pg_in[k].wait()
        start(pg.at[chunk(k), :, lanes(x2)], far.at[0, chunk(k)], FAR(k, 0), to_xm)
        start(pg.at[chunk(k), :, lanes(4 + x2)], far.at[1, chunk(k)], FAR(k, 1), to_xp)
    send_near(0)

    for s in range(SLOTS):
        r_in[s].wait()
        start(r_h.at[s, :, lanes(zo, HALF)], rf.at[s, own_rows, :], RZ(s), to_z)
    start(l_h.at[0], lp.at[0, pair_rows, :], LZ(0), to_z)

    def per_tile(k, step, unroll=2):
        def one(i, carry):
            step(k * PER + i)
            return carry

        lax.fori_loop(0, PER, one, 0, unroll=unroll)

    for k in range(CHUNKS):
        arrived(far.at[0, chunk(k)], FAR(k, 0))
        arrived(far.at[1, chunk(k)], FAR(k, 1))

        def add_chain(t):
            chs[0, t] = (
                far[0, t].astype(F32) + pg[t, :, lanes(xm)].astype(F32)
            ).astype(BF16)
            chs[1, t] = (
                far[1, t].astype(F32) + pg[t, :, lanes(4 + xp)].astype(F32)
            ).astype(BF16)

        per_tile(k, add_chain)
        if k + 1 < CHUNKS:
            send_near(k + 1)
        start(chs.at[0, chunk(k)], ch.at[0, chunk(k)], CHAIN(k, 0), to_xm)
        start(chs.at[1, chunk(k)], ch.at[1, chunk(k)], CHAIN(k, 1), to_xp)

    def total(half, t):
        return (
            pg[t, :, lanes(half * 4 + x)].astype(F32)
            + near[half, t].astype(F32)
            + ch[half, t].astype(F32)
        )

    for k in range(CHUNKS):
        for side in range(2):
            arrived(near.at[side, chunk(k)], NEAR(k, side))
            arrived(ch.at[side, chunk(k)], CHAIN(k, side))

        def other_half(t):
            hs[t] = total(zo, t).astype(BF16)

        per_tile(k, other_half)
        start(hs.at[chunk(k)], zrecv.at[chunk(k)], ZZ(k), to_z)

    def quad(chip, part, rows):
        return pl.ds(pl.multiple_of(chip * 256 + part, LANES), rows)

    for s in range(SLOTS):
        arrived(rf.at[s, own_rows, :], RZ(s))
        block = rf.at[s, quad(x, 0, 256), :]
        start(block, block, RN(s, 0), to_xp)
        start(block, block, RN(s, 1), to_xm)

    my_block = zl * 4 + x
    other_block = zo * 4 + x
    row_of = lax.broadcasted_iota(jnp.int32, (PIECE, COLS), 0) + me * PIECE
    col_of = lax.broadcasted_iota(jnp.int32, (PIECE, COLS), 1) + my_block * COLS
    for k in range(CHUNKS):
        arrived(zrecv.at[chunk(k)], ZZ(k))

        def share(t):
            rows, cols = extent(t)
            value = total(zl, t) + zrecv[t].astype(F32)
            shares[t] = jnp.where((row_of < rows) & (col_of < cols), value, 0.0).astype(BF16)

        per_tile(k, share)
    shares[TILES] = jnp.zeros((PIECE, COLS), BF16)

    my_cols = lanes(my_block)
    my_piece = pl.ds(pl.multiple_of(me * PIECE, PIECE), PIECE)
    for s in range(SLOTS):

        def stage(o, carry):
            staged[s, o] = shares[tile_s[s * OWNERS + o]]
            return carry

        lax.fori_loop(0, OWNERS, stage, 0, unroll=4)

    def to_owners(s):
        def one(k, carry):
            o = (me + k) % OWNERS
            pltpu.make_async_remote_copy(
                src_ref=staged.at[s, o],
                dst_ref=gf.at[s, my_piece, my_cols],
                send_sem=send.at[A2A(s)],
                recv_sem=recv.at[A2A(s)],
                device_id=owner_device(o),
                device_id_type=MESH,
            ).start()
            return carry

        lax.fori_loop(1, OWNERS, one, 0)

    for s in range(SLOTS):
        to_owners(s)
    for s in range(1, SLOTS):
        start(l_h.at[s], lp.at[s, pair_rows, :], LZ(s), to_z)
    for s in range(SLOTS):
        gf[s, my_piece, my_cols] = staged[s, me]

    def g_own(s):
        arrived(staged.at[s, pl.ds(0, OWNERS - 1)], A2A(s))
        block = gf.at[s, :, my_cols]
        start(block, block, GZ(s), to_z)
        start(block, block, GN(s, 0, 0), to_xp)
        start(block, block, GN(s, 1, 0), to_xm)

    def g_pair(s):
        block = gf.at[s, :, lanes(other_block)]
        arrived(block, GZ(s))
        start(block, block, GN(s, 0, 1), to_xp)
        start(block, block, GN(s, 1, 1), to_xm)

    def g_far(s):
        block = gf.at[s, :, lanes(xm)]
        arrived(block, GN(s, 0, zl))
        start(block, block, GF(s, 0), to_xp)
        block = gf.at[s, :, lanes(4 + xp)]
        arrived(block, GN(s, 1, zo))
        start(block, block, GF(s, 1), to_xm)

    def g_done(s):
        arrived(gf.at[s, :, lanes(4 + xm)], GN(s, 0, zo))
        arrived(gf.at[s, :, lanes(xp)], GN(s, 1, zl))
        arrived(gf.at[s, :, lanes(x2)], GF(s, 0))
        arrived(gf.at[s, :, lanes(4 + x2)], GF(s, 1))

    def r_far(s):
        arrived(rf.at[s, quad(xm, 0, 256), :], RN(s, 0))
        block = rf.at[s, quad(xm, 0, LANES), :]
        start(block, block, RF(s, 0), to_xp)
        arrived(rf.at[s, quad(xp, 0, 256), :], RN(s, 1))
        block = rf.at[s, quad(xp, LANES, LANES), :]
        start(block, block, RF(s, 1), to_xm)

    def r_done(s):
        arrived(rf.at[s, quad(x2, 0, LANES), :], RF(s, 0))
        arrived(rf.at[s, quad(x2, LANES, LANES), :], RF(s, 1))
        arrived(lp.at[s, pair_rows, :], LZ(s))

    def grams(s):
        gt[...] = gf[s, :, lanes(d)].T
        grad_rows = gf[s, pl.ds(pl.multiple_of(d * LANES, LANES), LANES), :]

        def columns(n, carry):
            at = pl.ds(pl.multiple_of(n * 256, 256), 256)
            right = jnp.dot(gt[...], gf[s, :, at], preferred_element_type=F32)
            nr[s, :, at] = stat_decay * rs[s, :, at] + (1.0 - stat_decay) * right
            part = jnp.dot(lp[s], gf[s, :, at], preferred_element_type=F32)
            tp[:, at] = part.astype(BF16)
            left = lax.dot_general(
                grad_rows, gf[s, at, :], (((1,), (1,)), ((), ())), preferred_element_type=F32
            )
            nl[s, :, at] = stat_decay * ls[s, :, at] + (1.0 - stat_decay) * left
            return carry

        lax.fori_loop(0, 4, columns, 0)

    outs = []

    def stats_out(s):
        for src, dst, sem in ((nl, nl_h, L_NL(s)), (nr, nr_h, L_NR(s))):
            copy = pltpu.make_async_copy(src.at[s], dst.at[s], local.at[sem])
            copy.start()
            outs.append(copy)

    out_cols = lanes(zl, HALF)

    def direction_rows(s):
        def columns(n, carry):
            at = pl.ds(pl.multiple_of(n * 256, 256), 256)
            obuf[:, at] = jnp.dot(tp[...], rf[s, :, at], preferred_element_type=F32)
            return carry

        lax.fori_loop(0, 2, columns, 0)

        def rows(i, carry):
            value = obuf[pl.ds(pl.multiple_of(i * 8, 8), 8), :]
            ostage[s, 2 * i] = value[:4].astype(BF16)
            ostage[s, 2 * i + 1] = value[4:].astype(BF16)
            return carry

        lax.fori_loop(0, 32, rows, 0, unroll=4)
        ret[s * OWNERS + me, :, out_cols] = ostage[s, here]

        def one(k, carry):
            i = (here + k) % 64
            pltpu.make_async_remote_copy(
                src_ref=ostage.at[s, i],
                dst_ref=ret.at[s * OWNERS + me, :, out_cols],
                send_sem=send.at[RET(s)],
                recv_sem=recv.at[RET(s)],
                device_id=any_device(i),
                device_id_type=MESH,
            ).start()
            return carry

        lax.fori_loop(1, 64, one, 0)

    g_own(0)
    for s in range(SLOTS):
        r_far(s)
    g_pair(0)
    g_own(1)
    g_far(0)
    g_pair(1)
    g_own(2)
    g_far(1)
    g_pair(2)
    for s in range(SLOTS):
        l_in[s].wait()
    ls_in.wait()
    rs_in.wait()
    g_done(0)
    r_done(0)
    grams(0)
    direction_rows(0)
    g_far(2)
    stats_out(0)
    g_done(1)
    r_done(1)
    grams(1)
    direction_rows(1)
    stats_out(1)
    g_done(2)
    r_done(2)
    grams(2)
    direction_rows(2)
    stats_out(2)

    for s in range(SLOTS):
        arrived(ostage.at[s, pl.ds(0, 63)], RET(s))
    line = lax.broadcasted_iota(jnp.int32, (4, TILE), 0) + (d * LANES + me * 4)
    lane = lax.broadcasted_iota(jnp.int32, (4, TILE), 1)

    def write(t, carry):
        rows, cols = extent(t)
        value = ret[place_s[t]].astype(F32)
        dir_o[t] = jnp.where((line < rows) & (lane < cols), value, 0.0).astype(BF16)
        return carry

    lax.fori_loop(0, TILES, write, 0, unroll=4)

    for copy in outs:
        copy.wait()
    for copy in sent:
        copy.wait_send()
    for s in range(SLOTS):
        for src, sem in (
            (staged.at[s, pl.ds(0, OWNERS - 1)], A2A(s)),
            (ostage.at[s, pl.ds(0, 63)], RET(s)),
        ):
            pltpu.make_async_remote_copy(
                src_ref=src,
                dst_ref=src,
                send_sem=send.at[sem],
                recv_sem=recv.at[sem],
                device_id=to_xp,
                device_id_type=MESH,
            ).wait_send()


def body(partial_grads, owner_map, left_stats, right_stats, left_roots, right_roots):
    ids = jnp.arange(TILES, dtype=jnp.int32)
    same = (owner_map[:, None] == owner_map[None, :]) & (ids[None, :] < ids[:, None])
    slot = jnp.sum(same.astype(jnp.int32), axis=1)
    place = slot * OWNERS + owner_map
    seats = jnp.arange(SLOTS * OWNERS, dtype=jnp.int32)
    tile_of = TILES + jnp.sum(
        jnp.where(place[None, :] == seats[:, None], ids[None, :] - TILES, 0), axis=1
    )
    smem = pl.BlockSpec(memory_space=pltpu.SMEM)
    hbm = pl.BlockSpec(memory_space=pl.ANY)
    direction, new_left, new_right = pl.pallas_call(
        kernel,
        out_shape=(
            jax.ShapeDtypeStruct((TILES, 4, TILE), BF16),
            jax.ShapeDtypeStruct((SLOTS, LANES, TILE), F32),
            jax.ShapeDtypeStruct((SLOTS, LANES, TILE), F32),
        ),
        in_specs=[smem, smem, hbm, hbm, hbm, hbm, hbm],
        out_specs=(pl.BlockSpec(memory_space=pltpu.VMEM), hbm, hbm),
        scratch_shapes=[
            pltpu.VMEM((TILES, PIECE, TILE), BF16),
            pltpu.VMEM((2, TILES, PIECE, COLS), BF16),
            pltpu.VMEM((2, TILES, PIECE, COLS), BF16),
            pltpu.VMEM((2, TILES, PIECE, COLS), BF16),
            pltpu.VMEM((2, TILES, PIECE, COLS), BF16),
            pltpu.VMEM((TILES, PIECE, COLS), BF16),
            pltpu.VMEM((TILES, PIECE, COLS), BF16),
            pltpu.VMEM((TILES + 1, PIECE, COLS), BF16),
            pltpu.VMEM((SLOTS, OWNERS, PIECE, COLS), BF16),
            pltpu.VMEM((SLOTS, TILE, TILE), BF16),
            pltpu.VMEM((SLOTS, TILE, HALF), BF16),
            pltpu.VMEM((SLOTS, 256, TILE), BF16),
            pltpu.VMEM((SLOTS, LANES, TILE), F32),
            pltpu.VMEM((SLOTS, LANES, TILE), F32),
            pltpu.VMEM((SLOTS, LANES, TILE), F32),
            pltpu.VMEM((SLOTS, LANES, TILE), F32),
            pltpu.VMEM((LANES, TILE), BF16),
            pltpu.VMEM((256, TILE), BF16),
            pltpu.VMEM((256, HALF), F32),
            pltpu.VMEM((SLOTS, 64, 4, HALF), BF16),
            pltpu.VMEM((SLOTS * OWNERS, 4, TILE), BF16),
            pltpu.SemaphoreType.DMA((N_SEMS,)),
            pltpu.SemaphoreType.DMA((N_SEMS,)),
            pltpu.SemaphoreType.DMA((N_LOC,)),
        ],
        compiler_params=pltpu.CompilerParams(
            collective_id=0, has_side_effects=True, vmem_limit_bytes=60 * 1024 * 1024
        ),
    )(
        tile_of,
        place,
        partial_grads[0],
        left_roots[0],
        right_roots[0],
        left_stats[0],
        right_stats[0],
    )
    return direction, new_left[None], new_right[None]


def solution(mesh):
    torus = Mesh(
        mesh.devices.reshape(4, 2, 4, 4, 2), ("dp_0", "dp_1", "owner_0", "owner_1", "owner_2")
    )
    in_specs = (
        P(DP, None, OWNER, None),
        P(),
        P(OWNER, None, DP, None),
        P(OWNER, None, DP, None),
        P(OWNER, None, DP, None),
        P(OWNER, None, DP, None),
    )
    out_specs = (P(None, DP_OWNER, None), P(OWNER, None, DP, None), P(OWNER, None, DP, None))
    return jax.shard_map(body, mesh=torus, in_specs=in_specs, out_specs=out_specs, check_vma=False)
```

time: 346 us -> 151 us (0.44)
  waiting for transfers between devices: 227 us -> 0 us
  Pallas kernels: 0 us -> 142 us
  blocking collectives: 42.6 us -> 0 us
  matrix products: 17.3 us -> 0 us
  starting transfers between devices: 16 us -> 0 us
  local copies, waits for them, and re-layouts: 20.8 us -> 5.87 us
  between operations: 14 us -> 0.64 us
  other arithmetic: 6.64 us -> 2.19 us
    all_gather x4 -> x0, waiting for transfers between devices: 163 us -> none  [gather_axes(): nearer = lax.all_gather(array, axes[-1], axis=dim, tiled=True)]
    pallas_call x0 -> x1, Pallas kernels: none -> 142 us  [body(): pl.pallas_call(kernel, out_shape=(jax.ShapeDtypeStruct((TILES, 4, TILE),...]
    all_to_all x2 -> x0, waiting for transfers between devices: 62.6 us -> none  [the longest x1 49.4 us: summed_on_arrival(): lax.all_to_all(parts, axis, split_axis=0, concat_axis=0, tiled=True)]
    all_to_all x2 -> x0, blocking collectives: 42.6 us -> none  [the longest x1 37.8 us: body(): lax.all_to_all(jnp.where(filled[:, :, None, None], taken, jnp.zeros((), s...]
    dot_general x3 -> x0, matrix products: 17.3 us -> none  [the longest x1 7.82 us: body(): jnp.einsum('srk,skc->src', left_part, gather_axes(right_roots[0], DP, 1),...]
    all_to_all x2 -> x0, starting transfers between devices: 15.7 us -> none  [the longest x1 9.33 us: moved_by_axis(): lax.all_to_all(parts, axes[k], split_axis=k, concat_axis=k, tiled=True)]
    transpose x2 -> x0, local copies, waits for them, and re-layouts: 4.41 us -> none  [the longest x1 4.12 us: cut_along(): return jnp.moveaxis(array.reshape(*before, count, -1, *after), dim, 0)]
    all_to_all x3 -> x0, local copies, waits for them, and re-layouts: 3.91 us -> none  [the longest x2 2.8 us: moved_by_axis(): lax.all_to_all(parts, axes[k], split_axis=k, concat_axis=k, tiled=True)]
  transfers between devices with their start and end apart: 6 -> 0, of which waited for: 5 -> 0; matrix products, arithmetic and copies ran while one was open for 6% -> 0% of each run, Pallas kernels for 0% -> 0%
where the time goes in v1:
time: 151 us
  Pallas kernels  142 us (94%)
  local copies, waits for them, and re-layouts  5.87 us (4%)
  other arithmetic  2.19 us (1%)
    pallas_call x1, Pallas kernels, body(): pl.pallas_call(kernel, out_shape=(jax.ShapeDtypeStruct((TILES, 4, TILE),...  142 us
    unnamed x7, local copies, waits for them, and re-layouts  5.87 us

profile of v1, /device:TPU:1, one launch (start us, length us, event | category | flops | bytes accessed | tf_op | source)
XLA Modules:
  0.0 151.1 jit_solution(9175280730725723093)
XLA Ops:
  0.6 0.9 convert_reduce_fusion
  1.5 0.7 iota_add_fusion
  2.2 0.0 copy-start.1
  2.2 0.1 select_reduce_fusion
  2.3 0.5 broadcast_add_fusion.tile_s
  2.8 0.0 copy-done.1
  2.8 142.4 %shard_map.85 = (bf16[48,4,1024]{2,1,0:T(4,128)(2,1)}, f32[3,128,1024]{2,1,0:T(8,128)}, f32[3,128,1024]{2,1,0:T(8,128)}) custom-call(s32[96]{0:T(128)} %broadcast_add_fusion.tile_s, s32[48]{0:T(128)} %copy-done.1, bf16[48,32,1024]{2,1,0:T(8,128)(2,1)} %bitcast.7, bf16[3,128,1024]{2,1,0:T(8,128)(2,1)} %bitcast.12, bf16[3,128,1024]{2,1,0:T(8,128)(2,1)} %bitcast.13, ...), custom_call_target="tpu_custom_call" | custom-call | tf_op jit(solution)/shard_map/pallas_call | solution.py:513
  145.3 1.9 %copy.12 = bf16[48,4,1024]{2,1,0:T(4,128)(2,1)} copy(bf16[48,4,1024]{2,1,0:T(4,128)(2,1)} %get-tuple-element.14) | data formatting | bytes 786432
  147.1 0.0 copy-start
  147.1 2.8 %copy.13 = f32[1,3,128,1024]{3,2,1,0:T(8,128)} copy(f32[1,3,128,1024]{3,2,1,0:T(8,128)} %bitcast.9) | data formatting | bytes 3145728
  150.0 0.0 copy-done
  150.0 1.1 copy.14
Async XLA Ops:
  2.2 0.6 copy-start.1
  147.1 2.9 %copy-start = (f32[3,128,1024]{2,1,0:T(8,128)S(1)}, f32[3,128,1024]{2,1,0:T(8,128)}, u32[]{:S(2)}) copy-start(f32[3,128,1024]{2,1,0:T(8,128)} %get-tuple-element.8) | copy-start | bytes 4718596

commit v2 on v1

--- a/solution.py
+++ b/solution.py
@@ -17,8 +17,8 @@
 LANES = 128
 COLS = 128
 HALF = 512
-CHUNKS = 4
-PER = TILES // CHUNKS
+BOUNDS = (0, 14, 28, 42, 48)
+CHUNKS = len(BOUNDS) - 1
 OWNER = ("owner_0", "owner_1", "owner_2")
 DP = ("dp_0", "dp_1")
 DP_OWNER = ("dp_0", "dp_1", "owner_0", "owner_1", "owner_2")
@@ -79,8 +79,11 @@
 LZ = IDS(SLOTS)
 A2A = IDS(SLOTS)
 GZ = IDS(SLOTS)
-GN = IDS(SLOTS, 2, 2)
+GZ_FAR = IDS(SLOTS)
+GN = IDS(SLOTS, 2)
+GP = IDS(SLOTS, 2, 2)
 GF = IDS(SLOTS, 2)
+GPF = IDS(SLOTS, 2)
 RET = IDS(SLOTS)
 N_SEMS = IDS.n
 LOC = Ids()
@@ -89,22 +92,20 @@
 L_L = LOC(SLOTS)
 L_LS = LOC(1)
 L_RS = LOC(1)
-L_NL = LOC(SLOTS)
-L_NR = LOC(SLOTS)
+L_SEAT = LOC(1)
 N_LOC = LOC.n
 
 
 def kernel(
-    tile_s,
-    place_s,
+    owner_s,
     pg_h,
     l_h,
     r_h,
     ls_h,
     rs_h,
-    dir_o,
-    nl_h,
-    nr_h,
+    ret,
+    nl,
+    nr,
     pg,
     far,
     chs,
@@ -119,13 +120,12 @@
     lp,
     ls,
     rs,
-    nl,
-    nr,
     gt,
     tp,
     obuf,
     ostage,
-    ret,
+    tile_v,
+    tile_s,
     send,
     recv,
     local,
@@ -185,7 +185,7 @@
         return pl.ds(pl.multiple_of(block * width, width), width)
 
     def chunk(k):
-        return pl.ds(k * PER, PER)
+        return pl.ds(BOUNDS[k], BOUNDS[k + 1] - BOUNDS[k])
 
     pg_in = [
         pltpu.make_async_copy(pg_h.at[chunk(k)], pg.at[chunk(k)], local.at[L_PG(k)])
@@ -221,6 +221,20 @@
         return carry
 
     lax.fori_loop(1, 64, greet, 0)
+
+    seat = lax.broadcasted_iota(jnp.int32, (1, LANES), 1)
+
+    def take(t, carry):
+        tile, count = carry
+        mine = seat % OWNERS == owner_s[t]
+        tile = jnp.where(mine & (count == seat // OWNERS), t, tile)
+        return tile, count + mine.astype(jnp.int32)
+
+    tile_v[...], _ = lax.fori_loop(
+        0, TILES, take, (jnp.full((1, LANES), TILES, jnp.int32), jnp.zeros((1, LANES), jnp.int32))
+    )
+    seats_in = pltpu.make_async_copy(tile_v, tile_s, local.at[L_SEAT(0)])
+    seats_in.start()
     pl.semaphore_wait(barrier, 65)
 
     def send_near(k):
@@ -236,14 +250,15 @@
     for s in range(SLOTS):
         r_in[s].wait()
         start(r_h.at[s, :, lanes(zo, HALF)], rf.at[s, own_rows, :], RZ(s), to_z)
-    start(l_h.at[0], lp.at[0, pair_rows, :], LZ(0), to_z)
-
-    def per_tile(k, step, unroll=2):
-        def one(i, carry):
-            step(k * PER + i)
+    for s in range(2):
+        start(l_h.at[s], lp.at[s, pair_rows, :], LZ(s), to_z)
+
+    def per_tile(k, step):
+        def one(t, carry):
+            step(t)
             return carry
 
-        lax.fori_loop(0, PER, one, 0, unroll=unroll)
+        lax.fori_loop(BOUNDS[k], BOUNDS[k + 1], one, 0, unroll=2)
 
     for k in range(CHUNKS):
         arrived(far.at[0, chunk(k)], FAR(k, 0))
@@ -263,6 +278,15 @@
         start(chs.at[0, chunk(k)], ch.at[0, chunk(k)], CHAIN(k, 0), to_xm)
         start(chs.at[1, chunk(k)], ch.at[1, chunk(k)], CHAIN(k, 1), to_xp)
 
+    def quad(chip, part, rows):
+        return pl.ds(pl.multiple_of(chip * 256 + part, LANES), rows)
+
+    for s in range(SLOTS):
+        arrived(rf.at[s, own_rows, :], RZ(s))
+        block = rf.at[s, quad(x, 0, 256), :]
+        start(block, block, RN(s, 0), to_xp)
+        start(block, block, RN(s, 1), to_xm)
+
     def total(half, t):
         return (
             pg[t, :, lanes(half * 4 + x)].astype(F32)
@@ -281,15 +305,6 @@
         per_tile(k, other_half)
         start(hs.at[chunk(k)], zrecv.at[chunk(k)], ZZ(k), to_z)
 
-    def quad(chip, part, rows):
-        return pl.ds(pl.multiple_of(chip * 256 + part, LANES), rows)
-
-    for s in range(SLOTS):
-        arrived(rf.at[s, own_rows, :], RZ(s))
-        block = rf.at[s, quad(x, 0, 256), :]
-        start(block, block, RN(s, 0), to_xp)
-        start(block, block, RN(s, 1), to_xm)
-
     my_block = zl * 4 + x
     other_block = zo * 4 + x
     row_of = lax.broadcasted_iota(jnp.int32, (PIECE, COLS), 0) + me * PIECE
@@ -307,10 +322,11 @@
 
     my_cols = lanes(my_block)
     my_piece = pl.ds(pl.multiple_of(me * PIECE, PIECE), PIECE)
+    seats_in.wait()
     for s in range(SLOTS):
 
         def stage(o, carry):
-            staged[s, o] = shares[tile_s[s * OWNERS + o]]
+            staged[s, o] = shares[tile_s[0, s * OWNERS + o]]
             return carry
 
         lax.fori_loop(0, OWNERS, stage, 0, unroll=4)
@@ -332,37 +348,62 @@
 
     for s in range(SLOTS):
         to_owners(s)
-    for s in range(1, SLOTS):
-        start(l_h.at[s], lp.at[s, pair_rows, :], LZ(s), to_z)
     for s in range(SLOTS):
         gf[s, my_piece, my_cols] = staged[s, me]
+
+    halves = (pl.ds(0, 512), pl.ds(512, 512))
 
     def g_own(s):
         arrived(staged.at[s, pl.ds(0, OWNERS - 1)], A2A(s))
         block = gf.at[s, :, my_cols]
         start(block, block, GZ(s), to_z)
-        start(block, block, GN(s, 0, 0), to_xp)
-        start(block, block, GN(s, 1, 0), to_xm)
+        start(block, block, GN(s, 0), to_xp)
+        start(block, block, GN(s, 1), to_xm)
 
     def g_pair(s):
-        block = gf.at[s, :, lanes(other_block)]
-        arrived(block, GZ(s))
-        start(block, block, GN(s, 0, 1), to_xp)
-        start(block, block, GN(s, 1, 1), to_xm)
+        arrived(gf.at[s, :, lanes(other_block)], GZ(s))
+        for turn in range(2):
+            block = gf.at[s, halves[turn], lanes(other_block)]
+            start(block, block, GP(s, 0, turn), to_xp)
+            block = gf.at[s, halves[1 - turn], lanes(other_block)]
+            start(block, block, GP(s, 1, turn), to_xm)
 
     def g_far(s):
-        block = gf.at[s, :, lanes(xm)]
-        arrived(block, GN(s, 0, zl))
+        arrived(gf.at[s, :, lanes(zl * 4 + xm)], GN(s, 0))
+        block = gf.at[s, halves[0], lanes(zl * 4 + xm)]
         start(block, block, GF(s, 0), to_xp)
-        block = gf.at[s, :, lanes(4 + xp)]
-        arrived(block, GN(s, 1, zo))
+        arrived(gf.at[s, :, lanes(zl * 4 + xp)], GN(s, 1))
+        block = gf.at[s, halves[1], lanes(zl * 4 + xp)]
         start(block, block, GF(s, 1), to_xm)
 
+    def g_far_pair(s):
+        arrived(gf.at[s, halves[0], lanes(zo * 4 + xm)], GP(s, 0, 0))
+        block = gf.at[s, halves[0], lanes(zo * 4 + xm)]
+        start(block, block, GPF(s, 0), to_xp)
+        arrived(gf.at[s, halves[1], lanes(zo * 4 + xp)], GP(s, 1, 0))
+        block = gf.at[s, halves[1], lanes(zo * 4 + xp)]
+        start(block, block, GPF(s, 1), to_xm)
+
+    def g_far_here(s):
+        arrived(gf.at[s, halves[0], lanes(zl * 4 + x2)], GF(s, 0))
+        arrived(gf.at[s, halves[1], lanes(zl * 4 + x2)], GF(s, 1))
+
+    def g_far_z(s):
+        g_far_here(s)
+        block = gf.at[s, :, lanes(zl * 4 + x2)]
+        start(block, block, GZ_FAR(s), to_z)
+
     def g_done(s):
-        arrived(gf.at[s, :, lanes(4 + xm)], GN(s, 0, zo))
-        arrived(gf.at[s, :, lanes(xp)], GN(s, 1, zl))
-        arrived(gf.at[s, :, lanes(x2)], GF(s, 0))
-        arrived(gf.at[s, :, lanes(4 + x2)], GF(s, 1))
+        if s < SLOTS - 1:
+            arrived(gf.at[s, halves[0], lanes(zo * 4 + xm)], GP(s, 0, 0))
+            arrived(gf.at[s, halves[1], lanes(zo * 4 + xp)], GP(s, 1, 0))
+        arrived(gf.at[s, halves[1], lanes(zo * 4 + xm)], GP(s, 0, 1))
+        arrived(gf.at[s, halves[0], lanes(zo * 4 + xp)], GP(s, 1, 1))
+        if s < SLOTS - 1:
+            arrived(gf.at[s, :, lanes(zo * 4 + x2)], GZ_FAR(s))
+        else:
+            arrived(gf.at[s, halves[0], lanes(zo * 4 + x2)], GPF(s, 0))
+            arrived(gf.at[s, halves[1], lanes(zo * 4 + x2)], GPF(s, 1))
 
     def r_far(s):
         arrived(rf.at[s, quad(xm, 0, 256), :], RN(s, 0))
@@ -385,8 +426,6 @@
             at = pl.ds(pl.multiple_of(n * 256, 256), 256)
             right = jnp.dot(gt[...], gf[s, :, at], preferred_element_type=F32)
             nr[s, :, at] = stat_decay * rs[s, :, at] + (1.0 - stat_decay) * right
-            part = jnp.dot(lp[s], gf[s, :, at], preferred_element_type=F32)
-            tp[:, at] = part.astype(BF16)
             left = lax.dot_general(
                 grad_rows, gf[s, at, :], (((1,), (1,)), ((), ())), preferred_element_type=F32
             )
@@ -395,15 +434,16 @@
 
         lax.fori_loop(0, 4, columns, 0)
 
-    outs = []
-
-    def stats_out(s):
-        for src, dst, sem in ((nl, nl_h, L_NL(s)), (nr, nr_h, L_NR(s))):
-            copy = pltpu.make_async_copy(src.at[s], dst.at[s], local.at[sem])
-            copy.start()
-            outs.append(copy)
-
     out_cols = lanes(zl, HALF)
+
+    def left_part(s, half):
+        def columns(n, carry):
+            at = pl.ds(pl.multiple_of(half * HALF + n * 256, 256), 256)
+            part = jnp.dot(lp[s], gf[s, :, at], preferred_element_type=F32)
+            tp[:, at] = part.astype(BF16)
+            return carry
+
+        lax.fori_loop(0, 2, columns, 0)
 
     def direction_rows(s):
         def columns(n, carry):
@@ -413,75 +453,79 @@
 
         lax.fori_loop(0, 2, columns, 0)
 
-        def rows(i, carry):
+        def rows(i):
             value = obuf[pl.ds(pl.multiple_of(i * 8, 8), 8), :]
             ostage[s, 2 * i] = value[:4].astype(BF16)
             ostage[s, 2 * i + 1] = value[4:].astype(BF16)
-            return carry
-
-        lax.fori_loop(0, 32, rows, 0, unroll=4)
-        ret[s * OWNERS + me, :, out_cols] = ostage[s, here]
-
-        def one(k, carry):
-            i = (here + k) % 64
+
+        def give(i, core):
             pltpu.make_async_remote_copy(
-                src_ref=ostage.at[s, i],
+                src_ref=ostage.at[s, 2 * i + core],
                 dst_ref=ret.at[s * OWNERS + me, :, out_cols],
                 send_sem=send.at[RET(s)],
                 recv_sem=recv.at[RET(s)],
-                device_id=any_device(i),
+                device_id={
+                    "dp_1": i // 16,
+                    "owner_0": (i // 4) % 4,
+                    "owner_1": i % 4,
+                    "owner_2": core,
+                },
                 device_id_type=MESH,
             ).start()
+
+        chip = here // 2
+        rows((chip + 1) % 32)
+
+        def one(k, carry):
+            rows((chip + k + 1) % 32)
+            give((chip + k) % 32, 0)
+            give((chip + k) % 32, 1)
             return carry
 
-        lax.fori_loop(1, 64, one, 0)
+        lax.fori_loop(1, 32, one, 0)
+        ret[s * OWNERS + me, :, out_cols] = ostage[s, here]
+        give(chip, 1 - co)
 
     g_own(0)
     for s in range(SLOTS):
         r_far(s)
+    g_own(1)
+    g_own(2)
     g_pair(0)
-    g_own(1)
+    start(l_h.at[2], lp.at[2, pair_rows, :], LZ(2), to_z)
     g_far(0)
     g_pair(1)
-    g_own(2)
     g_far(1)
     g_pair(2)
+    g_far(2)
+    g_far_z(0)
+    g_far_z(1)
     for s in range(SLOTS):
         l_in[s].wait()
     ls_in.wait()
     rs_in.wait()
     g_done(0)
     r_done(0)
+    left_part(0, 0)
+    left_part(0, 1)
+    direction_rows(0)
+    g_far_pair(2)
     grams(0)
-    direction_rows(0)
-    g_far(2)
-    stats_out(0)
     g_done(1)
     r_done(1)
+    left_part(1, 0)
+    left_part(1, 1)
+    direction_rows(1)
     grams(1)
-    direction_rows(1)
-    stats_out(1)
+    r_done(2)
+    g_far_here(2)
+    left_part(2, zl)
     g_done(2)
-    r_done(2)
+    left_part(2, zo)
+    direction_rows(2)
     grams(2)
-    direction_rows(2)
-    stats_out(2)
-
     for s in range(SLOTS):
         arrived(ostage.at[s, pl.ds(0, 63)], RET(s))
-    line = lax.broadcasted_iota(jnp.int32, (4, TILE), 0) + (d * LANES + me * 4)
-    lane = lax.broadcasted_iota(jnp.int32, (4, TILE), 1)
-
-    def write(t, carry):
-        rows, cols = extent(t)
-        value = ret[place_s[t]].astype(F32)
-        dir_o[t] = jnp.where((line < rows) & (lane < cols), value, 0.0).astype(BF16)
-        return carry
-
-    lax.fori_loop(0, TILES, write, 0, unroll=4)
-
-    for copy in outs:
-        copy.wait()
     for copy in sent:
         copy.wait_send()
     for s in range(SLOTS):
@@ -499,26 +543,53 @@
             ).wait_send()
 
 
+def write_out(owner_s, ret, nl, nr, dir_h, nl_h, nr_h, rows_v, count_s, sems):
+    copies = [
+        pltpu.make_async_copy(nl, nl_h, sems.at[0]),
+        pltpu.make_async_copy(nr, nr_h, sems.at[1]),
+    ]
+    for copy in copies:
+        copy.start()
+    d = lax.axis_index(DP)
+    me = lax.axis_index(OWNER)
+    line = lax.broadcasted_iota(jnp.int32, (4, TILE), 0) + (d * LANES + me * 4)
+    lane = lax.broadcasted_iota(jnp.int32, (4, TILE), 1)
+
+    def clear(o, carry):
+        count_s[o] = 0
+        return carry
+
+    lax.fori_loop(0, OWNERS, clear, 0, unroll=8)
+
+    def write(t, carry):
+        rows, cols = extent(t)
+        owner = owner_s[t]
+        taken = count_s[owner]
+        count_s[owner] = taken + OWNERS
+        value = ret[taken + owner].astype(F32)
+        rows_v[t] = jnp.where((line < rows) & (lane < cols), value, 0.0).astype(BF16)
+        return carry
+
+    lax.fori_loop(0, TILES, write, 0, unroll=4)
+    copies.append(pltpu.make_async_copy(rows_v, dir_h, sems.at[2]))
+    copies[2].start()
+    for copy in copies:
+        copy.wait()
+
+
 def body(partial_grads, owner_map, left_stats, right_stats, left_roots, right_roots):
-    ids = jnp.arange(TILES, dtype=jnp.int32)
-    same = (owner_map[:, None] == owner_map[None, :]) & (ids[None, :] < ids[:, None])
-    slot = jnp.sum(same.astype(jnp.int32), axis=1)
-    place = slot * OWNERS + owner_map
-    seats = jnp.arange(SLOTS * OWNERS, dtype=jnp.int32)
-    tile_of = TILES + jnp.sum(
-        jnp.where(place[None, :] == seats[:, None], ids[None, :] - TILES, 0), axis=1
-    )
     smem = pl.BlockSpec(memory_space=pltpu.SMEM)
-    hbm = pl.BlockSpec(memory_space=pl.ANY)
-    direction, new_left, new_right = pl.pallas_call(
+    vmem = pl.BlockSpec(memory_space=pltpu.VMEM)
+    hbm = pl.BlockSpec(memory_space=pltpu.HBM)
+    returned, new_left, new_right = pl.pallas_call(
         kernel,
         out_shape=(
-            jax.ShapeDtypeStruct((TILES, 4, TILE), BF16),
-            jax.ShapeDtypeStruct((SLOTS, LANES, TILE), F32),
-            jax.ShapeDtypeStruct((SLOTS, LANES, TILE), F32),
+            pltpu.VMEM((SLOTS * OWNERS, 4, TILE), BF16),
+            pltpu.VMEM((SLOTS, LANES, TILE), F32),
+            pltpu.VMEM((SLOTS, LANES, TILE), F32),
         ),
-        in_specs=[smem, smem, hbm, hbm, hbm, hbm, hbm],
-        out_specs=(pl.BlockSpec(memory_space=pltpu.VMEM), hbm, hbm),
+        in_specs=[smem, hbm, hbm, hbm, hbm, hbm],
+        out_specs=(vmem, vmem, vmem),
         scratch_shapes=[
             pltpu.VMEM((TILES, PIECE, TILE), BF16),
             pltpu.VMEM((2, TILES, PIECE, COLS), BF16),
@@ -534,13 +605,12 @@
             pltpu.VMEM((SLOTS, 256, TILE), BF16),
             pltpu.VMEM((SLOTS, LANES, TILE), F32),
             pltpu.VMEM((SLOTS, LANES, TILE), F32),
-            pltpu.VMEM((SLOTS, LANES, TILE), F32),
-            pltpu.VMEM((SLOTS, LANES, TILE), F32),
             pltpu.VMEM((LANES, TILE), BF16),
             pltpu.VMEM((256, TILE), BF16),
             pltpu.VMEM((256, HALF), F32),
             pltpu.VMEM((SLOTS, 64, 4, HALF), BF16),
-            pltpu.VMEM((SLOTS * OWNERS, 4, TILE), BF16),
+            pltpu.VMEM((1, LANES), jnp.int32),
+            pltpu.SMEM((1, LANES), jnp.int32),
             pltpu.SemaphoreType.DMA((N_SEMS,)),
             pltpu.SemaphoreType.DMA((N_SEMS,)),
             pltpu.SemaphoreType.DMA((N_LOC,)),
@@ -549,13 +619,34 @@
             collective_id=0, has_side_effects=True, vmem_limit_bytes=60 * 1024 * 1024
         ),
     )(
-        tile_of,
-        place,
+        owner_map,
         partial_grads[0],
         left_roots[0],
         right_roots[0],
         left_stats[0],
         right_stats[0],
+    )
+    direction, new_left, new_right = pl.pallas_call(
+        write_out,
+        out_shape=(
+            jax.ShapeDtypeStruct((TILES, 4, TILE), BF16),
+            jax.ShapeDtypeStruct((SLOTS, LANES, TILE), F32),
+            jax.ShapeDtypeStruct((SLOTS, LANES, TILE), F32),
+        ),
+        in_specs=[smem, vmem, vmem, vmem],
+        out_specs=(hbm, hbm, hbm),
+        scratch_shapes=[
+            pltpu.VMEM((TILES, 4, TILE), BF16),
+            pltpu.SMEM((OWNERS,), jnp.int32),
+            pltpu.SemaphoreType.DMA((3,)),
+        ],
+        compiler_params=pltpu.CompilerParams(vmem_limit_bytes=4 * 1024 * 1024),
+    )(
+        owner_map,
+        *(
+            pltpu.with_memory_space_constraint(value, pltpu.VMEM)
+            for value in (returned, new_left, new_right)
+        ),
     )
     return direction, new_left[None], new_right[None]
 

time: 151 us -> 133 us (0.88)
  Pallas kernels: 142 us -> 133 us
  local copies, waits for them, and re-layouts: 5.87 us -> 0.01 us
  other arithmetic: 2.19 us -> 0 us
    pallas_call x1 -> x2, Pallas kernels: 142 us -> 133 us  [the longest x1 130 us: body(): pl.pallas_call(kernel, out_shape=(pltpu.VMEM((SLOTS * OWNERS, 4, TILE), B...]
    unnamed x7 -> x2, local copies, waits for them, and re-layouts: 5.87 us -> 0.01 us
where the time goes in v2:
time: 133 us
  Pallas kernels  133 us (100%)
    pallas_call x1, Pallas kernels, body(): pl.pallas_call(kernel, out_shape=(pltpu.VMEM((SLOTS * OWNERS, 4, TILE), B...  130 us

profile of v2, /device:TPU:1, one launch (start us, length us, event | category | flops | bytes accessed | tf_op | source)
XLA Modules:
  0.0 133.3 jit_solution(9131933139922136828)
XLA Ops:
  0.6 0.0 copy-start
  0.6 130.3 %shard_map.85 = (bf16[96,4,1024]{2,1,0:T(4,128)(2,1)S(1)}, f32[3,128,1024]{2,1,0:T(8,128)S(1)}, f32[3,128,1024]{2,1,0:T(8,128)S(1)}) custom-call(s32[48]{0:T(128)} %owner_s.3, bf16[48,32,1024]{2,1,0:T(8,128)(2,1)} %bitcast.7, bf16[3,128,1024]{2,1,0:T(8,128)(2,1)} %bitcast.10, bf16[3,128,1024]{2,1,0:T(8,128)(2,1)} %bitcast.11, f32[3,128,1024]{2,1,0:T(8,128)} %bitcast.8, ...), custom_call_target="tpu_custom_call" | custom-call | tf_op jit(solution)/shard_map/pallas_call | solution.py:584
  131.0 0.0 copy-done
  131.0 2.3 %shard_map.86 = (bf16[48,4,1024]{2,1,0:T(4,128)(2,1)}, f32[3,128,1024]{2,1,0:T(8,128)}, f32[3,128,1024]{2,1,0:T(8,128)}) custom-call(s32[48]{0:T(128)S(1)} %copy-done, bf16[96,4,1024]{2,1,0:T(4,128)(2,1)S(1)} %get-tuple-element.9.ret, f32[3,128,1024]{2,1,0:T(8,128)S(1)} %get-tuple-element.10.nl, f32[3,128,1024]{2,1,0:T(8,128)S(1)} %get-tuple-element.11.nr), custom_call_target="tpu_custom_call" | custom-call | tf_op jit(solution)/shard_map/pallas_call | solution.py:629
Async XLA Ops:
  0.6 130.3 %copy-start = (s32[48]{0:T(128)S(1)}, s32[48]{0:T(128)}, u32[]{:S(2)}) copy-start(s32[48]{0:T(128)} %owner_s.3) | copy-start | bytes 580

commit v3 on v2

--- a/solution.py
+++ b/solution.py
@@ -129,6 +129,7 @@
     send,
     recv,
     local,
+    told,
 ):
     x = lax.axis_index("dp_0")
     zl = lax.axis_index("dp_1")
@@ -211,16 +212,12 @@
         copy.start()
 
     barrier = pltpu.get_barrier_semaphore()
-    pl.semaphore_signal(barrier, inc=1, device_id=to_xp, device_id_type=MESH)
-    pl.semaphore_signal(barrier, inc=1, device_id=to_xm, device_id_type=MESH)
-
-    def greet(k, carry):
-        pl.semaphore_signal(
-            barrier, inc=1, device_id=any_device((here + k) % 64), device_id_type=MESH
-        )
-        return carry
-
-    lax.fori_loop(1, 64, greet, 0)
+    to_core = {"owner_2": 1 - co}
+    y_sides = ({"owner_0": (y + 1) % 4}, {"owner_0": (y + 3) % 4})
+    zh_sides = ({"owner_1": (zh + 1) % 4}, {"owner_1": (zh + 3) % 4})
+    neighbours = (to_xp, to_xm, to_z, to_core, *y_sides, *zh_sides)
+    for device in neighbours:
+        pl.semaphore_signal(barrier, inc=1, device_id=device, device_id_type=MESH)
 
     seat = lax.broadcasted_iota(jnp.int32, (1, LANES), 1)
 
@@ -235,7 +232,16 @@
     )
     seats_in = pltpu.make_async_copy(tile_v, tile_s, local.at[L_SEAT(0)])
     seats_in.start()
-    pl.semaphore_wait(barrier, 65)
+    pl.semaphore_wait(barrier, len(neighbours))
+
+    rounds = (y_sides, zh_sides, zh_sides, (to_core,), (to_z,))
+
+    def tell(n):
+        for device in rounds[n]:
+            pl.semaphore_signal(told.at[n], inc=1, device_id=device, device_id_type=MESH)
+
+    def heard(n):
+        pl.semaphore_wait(told.at[n], len(rounds[n]))
 
     def send_near(k):
         start(pg.at[chunk(k), :, lanes(xp)], near.at[0, chunk(k)], NEAR(k, 0), to_xp)
@@ -246,6 +252,7 @@
         start(pg.at[chunk(k), :, lanes(x2)], far.at[0, chunk(k)], FAR(k, 0), to_xm)
         start(pg.at[chunk(k), :, lanes(4 + x2)], far.at[1, chunk(k)], FAR(k, 1), to_xp)
     send_near(0)
+    tell(0)
 
     for s in range(SLOTS):
         r_in[s].wait()
@@ -275,6 +282,8 @@
         per_tile(k, add_chain)
         if k + 1 < CHUNKS:
             send_near(k + 1)
+        heard(k)
+        tell(k + 1)
         start(chs.at[0, chunk(k)], ch.at[0, chunk(k)], CHAIN(k, 0), to_xm)
         start(chs.at[1, chunk(k)], ch.at[1, chunk(k)], CHAIN(k, 1), to_xp)
 
@@ -346,6 +355,7 @@
 
         lax.fori_loop(1, OWNERS, one, 0)
 
+    heard(4)
     for s in range(SLOTS):
         to_owners(s)
     for s in range(SLOTS):
@@ -516,13 +526,13 @@
     left_part(1, 0)
     left_part(1, 1)
     direction_rows(1)
-    grams(1)
     r_done(2)
     g_far_here(2)
     left_part(2, zl)
     g_done(2)
     left_part(2, zo)
     direction_rows(2)
+    grams(1)
     grams(2)
     for s in range(SLOTS):
         arrived(ostage.at[s, pl.ds(0, 63)], RET(s))
@@ -614,6 +624,7 @@
             pltpu.SemaphoreType.DMA((N_SEMS,)),
             pltpu.SemaphoreType.DMA((N_SEMS,)),
             pltpu.SemaphoreType.DMA((N_LOC,)),
+            pltpu.SemaphoreType.REGULAR((5,)),
         ],
         compiler_params=pltpu.CompilerParams(
             collective_id=0, has_side_effects=True, vmem_limit_bytes=60 * 1024 * 1024

time: 133 us -> 129 us (0.970)
  Pallas kernels: 133 us -> 128 us
    pallas_call x1, Pallas kernels: 130 us -> 125 us  [body(): pl.pallas_call(kernel, out_shape=(pltpu.VMEM((SLOTS * OWNERS, 4, TILE), B...]
where the time goes in v3:
time: 129 us; the launch traced here: 128 us
  Pallas kernels  128 us (99%)
    pallas_call x1, Pallas kernels, body(): pl.pallas_call(kernel, out_shape=(pltpu.VMEM((SLOTS * OWNERS, 4, TILE), B...  125 us

profile of v3, /device:TPU:1, one launch (start us, length us, event | category | flops | bytes accessed | tf_op | source)
XLA Modules:
  0.0 128.5 jit_solution(18360563485147554216)
XLA Ops:
  0.6 0.0 copy-start
  0.6 125.5 %shard_map.85 = (bf16[96,4,1024]{2,1,0:T(4,128)(2,1)S(1)}, f32[3,128,1024]{2,1,0:T(8,128)S(1)}, f32[3,128,1024]{2,1,0:T(8,128)S(1)}) custom-call(s32[48]{0:T(128)} %owner_s.3, bf16[48,32,1024]{2,1,0:T(8,128)(2,1)} %bitcast.7, bf16[3,128,1024]{2,1,0:T(8,128)(2,1)} %bitcast.10, bf16[3,128,1024]{2,1,0:T(8,128)(2,1)} %bitcast.11, f32[3,128,1024]{2,1,0:T(8,128)} %bitcast.8, ...), custom_call_target="tpu_custom_call" | custom-call | tf_op jit(solution)/shard_map/pallas_call | solution.py:594
  126.1 0.0 copy-done
  126.1 2.3 %shard_map.86 = (bf16[48,4,1024]{2,1,0:T(4,128)(2,1)}, f32[3,128,1024]{2,1,0:T(8,128)}, f32[3,128,1024]{2,1,0:T(8,128)}) custom-call(s32[48]{0:T(128)S(1)} %copy-done, bf16[96,4,1024]{2,1,0:T(4,128)(2,1)S(1)} %get-tuple-element.9.ret, f32[3,128,1024]{2,1,0:T(8,128)S(1)} %get-tuple-element.10.nl, f32[3,128,1024]{2,1,0:T(8,128)S(1)} %get-tuple-element.11.nr), custom_call_target="tpu_custom_call" | custom-call | tf_op jit(solution)/shard_map/pallas_call | solution.py:640
Async XLA Ops:
  0.6 125.5 %copy-start = (s32[48]{0:T(128)S(1)}, s32[48]{0:T(128)}, u32[]{:S(2)}) copy-start(s32[48]{0:T(128)} %owner_s.3) | copy-start | bytes 580

commit v4 on v3

--- a/solution.py
+++ b/solution.py
@@ -356,17 +356,20 @@
         lax.fori_loop(1, OWNERS, one, 0)
 
     heard(4)
-    for s in range(SLOTS):
-        to_owners(s)
+    to_owners(0)
+    to_owners(1)
     for s in range(SLOTS):
         gf[s, my_piece, my_cols] = staged[s, me]
 
     halves = (pl.ds(0, 512), pl.ds(512, 512))
 
-    def g_own(s):
+    def g_here(s):
         arrived(staged.at[s, pl.ds(0, OWNERS - 1)], A2A(s))
         block = gf.at[s, :, my_cols]
         start(block, block, GZ(s), to_z)
+
+    def g_own(s):
+        block = gf.at[s, :, my_cols]
         start(block, block, GN(s, 0), to_xp)
         start(block, block, GN(s, 1), to_xm)
 
@@ -496,20 +499,23 @@
         ret[s * OWNERS + me, :, out_cols] = ostage[s, here]
         give(chip, 1 - co)
 
+    g_here(0)
     g_own(0)
-    for s in range(SLOTS):
-        r_far(s)
+    to_owners(2)
+    r_far(0)
+    r_far(1)
+    r_far(2)
+    g_pair(0)
+    g_far(0)
+    g_here(1)
     g_own(1)
+    g_pair(1)
+    g_here(2)
+    g_far_z(0)
+    start(l_h.at[2], lp.at[2, pair_rows, :], LZ(2), to_z)
+    g_far(1)
     g_own(2)
-    g_pair(0)
-    start(l_h.at[2], lp.at[2, pair_rows, :], LZ(2), to_z)
-    g_far(0)
-    g_pair(1)
-    g_far(1)
     g_pair(2)
-    g_far(2)
-    g_far_z(0)
-    g_far_z(1)
     for s in range(SLOTS):
         l_in[s].wait()
     ls_in.wait()
@@ -519,20 +525,22 @@
     left_part(0, 0)
     left_part(0, 1)
     direction_rows(0)
+    grams(0)
+    g_far_z(1)
+    g_far(2)
     g_far_pair(2)
-    grams(0)
     g_done(1)
     r_done(1)
     left_part(1, 0)
     left_part(1, 1)
     direction_rows(1)
+    grams(1)
     r_done(2)
     g_far_here(2)
     left_part(2, zl)
     g_done(2)
     left_part(2, zo)
     direction_rows(2)
-    grams(1)
     grams(2)
     for s in range(SLOTS):
         arrived(ostage.at[s, pl.ds(0, 63)], RET(s))

time: 129 us -> 124 us (0.961)
  Pallas kernels: 128 us -> 123 us
    pallas_call x1, Pallas kernels: 125 us -> 121 us  [body(): pl.pallas_call(kernel, out_shape=(pltpu.VMEM((SLOTS * OWNERS, 4, TILE), B...]
where the time goes in v4:
time: 124 us
  Pallas kernels  123 us (99%)
    pallas_call x1, Pallas kernels, body(): pl.pallas_call(kernel, out_shape=(pltpu.VMEM((SLOTS * OWNERS, 4, TILE), B...  121 us

profile of v4, /device:TPU:1, one launch (start us, length us, event | category | flops | bytes accessed | tf_op | source)
XLA Modules:
  0.0 123.6 jit_solution(3522900135417085632)
XLA Ops:
  0.6 0.0 copy-start
  0.6 120.6 %shard_map.85 = (bf16[96,4,1024]{2,1,0:T(4,128)(2,1)S(1)}, f32[3,128,1024]{2,1,0:T(8,128)S(1)}, f32[3,128,1024]{2,1,0:T(8,128)S(1)}) custom-call(s32[48]{0:T(128)} %owner_s.3, bf16[48,32,1024]{2,1,0:T(8,128)(2,1)} %bitcast.7, bf16[3,128,1024]{2,1,0:T(8,128)(2,1)} %bitcast.10, bf16[3,128,1024]{2,1,0:T(8,128)(2,1)} %bitcast.11, f32[3,128,1024]{2,1,0:T(8,128)} %bitcast.8, ...), custom_call_target="tpu_custom_call" | custom-call | tf_op jit(solution)/shard_map/pallas_call | solution.py:602
  121.2 0.0 copy-done
  121.2 2.3 %shard_map.86 = (bf16[48,4,1024]{2,1,0:T(4,128)(2,1)}, f32[3,128,1024]{2,1,0:T(8,128)}, f32[3,128,1024]{2,1,0:T(8,128)}) custom-call(s32[48]{0:T(128)S(1)} %copy-done, bf16[96,4,1024]{2,1,0:T(4,128)(2,1)S(1)} %get-tuple-element.9.ret, f32[3,128,1024]{2,1,0:T(8,128)S(1)} %get-tuple-element.10.nl, f32[3,128,1024]{2,1,0:T(8,128)S(1)} %get-tuple-element.11.nr), custom_call_target="tpu_custom_call" | custom-call | tf_op jit(solution)/shard_map/pallas_call | solution.py:648
Async XLA Ops:
  0.6 120.6 %copy-start = (s32[48]{0:T(128)S(1)}, s32[48]{0:T(128)}, u32[]{:S(2)}) copy-start(s32[48]{0:T(128)} %owner_s.3) | copy-start | bytes 580
